TPU v7x, 128 devices: a whole 4x4x4 slice. The times are simulated.
128 devices in a mesh: lat: 8 (over y, core), lon: 4 (over x), lev: 4 (over z).
Axes of the slice: x: 4, y: 4, z: 4, core: 2. Of those that a mesh axis runs over, the one named last changes fastest.
Arguments:
- tracer: float32 [32, 512, 128, 128], P('lat', 'lon', 'lev'), may hold values from 0.5 to 2
- conductance: float32 [32, 512, 128, 128], P('lat', 'lon', 'lev'), may hold values from 0.03 to 0.15
- source: float32 [32, 512, 128, 128], P('lat', 'lon', 'lev'), may hold values from -0.2 to 0.2
Outputs:
- standardized: float32 [32, 512, 128, 128], P('lat', 'lon', 'lev')
- tracer_end: float32 [32, 512, 128, 128], P('lat', 'lon', 'lev')
All inputs are finite; a program needn't handle non-finite values.
Results may differ from a plain program's by a relative error of at most 0.00002.
Values sent between devices are 32-bit elements; how exact they have to be, the bound alone decides.
A program may use at most 128 MiB of HBM per device.

v0:
```python
import functools

import jax
import jax.numpy as jnp
from jax import lax
from jax.experimental import pallas as pl
from jax.experimental.pallas import tpu as pltpu
from jax.sharding import PartitionSpec as P

STEPS = 3
ROWS = 8
MESH = pl.DeviceIdType.MESH


def sweep(length, groups, total, centre, near, far, low, high, before, after, held, added, store, sums):
    row = lax.broadcasted_iota(jnp.int32, (ROWS, 128), 0)
    first, last = row == 0, row == ROWS - 1

    def block(t, carry, closing):
        previous, current, so_far = carry
        base = t * ROWS if closing else pl.multiple_of(t * ROWS, ROWS)
        lows = low(base) if 0 in groups else None
        highs = high(base) if total - 1 in groups else None
        for q in range(ROWS):
            i = base + q
            if closing and q == ROWS - 1:
                following = [after(g) for g in groups]
            else:
                following = [centre(i + 1, g) for g in groups]
            row_of = dict(zip(groups, current))
            for g in (groups[0] - 1, groups[-1] + 1):
                if 0 <= g < total:
                    row_of[g] = centre(i, g)
            down = {g: pltpu.roll(v, 1, 0) for g, v in row_of.items() if g <= groups[-1]}
            up = {g: pltpu.roll(v, ROWS - 1, 0) for g, v in row_of.items() if g >= groups[0]}
            if lows is not None:
                down[-1] = jnp.broadcast_to(lows[q : q + 1], (ROWS, 128))
            if highs is not None:
                up[total] = jnp.broadcast_to(highs[q : q + 1], (ROWS, 128))
            done = []
            for n, g in enumerate(groups):
                lower = jnp.where(first, down[g - 1], down[g])
                upper = jnp.where(last, up[g + 1], up[g])
                spread = (lower + upper) + (previous[n] + following[n]) + (near(i, g) + far(i, g))
                spread = spread - 6.0 * current[n]
                value = current[n] + held(i, g) * spread + added(i, g)
                store(i, g, value)
                done.append(value)
            if sums:
                so_far = [a + b for a, b in zip(so_far, done)]
            previous, current = current, following
        return previous, current, so_far

    zeros = [jnp.zeros((ROWS, 128), jnp.float32) for _ in groups] if sums else []
    carry = ([before(g) for g in groups], [centre(0, g) for g in groups], zeros)
    blocks = length // ROWS
    carry = lax.fori_loop(0, blocks - 1, lambda t, c: block(t, c, False), carry)
    return block(blocks - 1, carry, True)[2]


def along(length, body, carry, unroll=8):
    def block(t, carry):
        for q in range(unroll):
            carry = body(t * unroll + q, carry)
        return carry

    return lax.fori_loop(0, length // unroll, block, carry)


def march(
    sizes,
    tracer,
    conductance,
    source,
    end,
    scaled,
    even,
    odd,
    chip,
    pair,
    edge_k,
    edge_i,
    mine,
    theirs,
    mine_0,
    theirs_0,
    load_sem,
    chip_send,
    chip_recv,
    pair_send,
    pair_recv,
    k_send,
    k_recv,
    i_send,
    i_recv,
    sum_send,
    sum_recv,
    sum_0_send,
    sum_0_recv,
):
    n_lat, n_lon, n_lev = sizes
    planes, length, depth, _ = tracer.shape
    groups = list(range(depth // ROWS))
    total = len(groups)
    lat, lon, lev = (lax.axis_index(a) for a in ("lat", "lon", "lev"))
    core = lax.rem(lat, 2)
    way = 1 - 2 * core
    first = core * (planes - 1)
    rest = 1 - core
    partner = lat + way
    peer = lat - way
    has_peer = jnp.logical_and(peer >= 0, peer < n_lat)
    others = planes - 1

    def plane(p):
        return first + way * p

    def rows(g):
        return pl.ds(ROWS * g, ROWS)

    def load(n, p):
        a, b = ((tracer, even), (conductance, scaled), (source, end))[n]
        return pltpu.make_async_copy(a.at[plane(p)], b.at[plane(p)], load_sem.at[n, p])

    for n in range(3):
        for p in (*range(1, planes), 0):
            load(n, p).start()

    barrier = pltpu.get_barrier_semaphore()
    pl.semaphore_signal(barrier, 1, device_id={"lat": partner}, device_id_type=MESH)

    @pl.when(has_peer)
    def _():
        pl.semaphore_signal(barrier, 1, device_id={"lat": peer}, device_id_type=MESH)

    @pl.when(lev > 0)
    def _():
        pl.semaphore_signal(barrier, 1, device_id={"lev": lev - 1}, device_id_type=MESH)

    @pl.when(lev < n_lev - 1)
    def _():
        pl.semaphore_signal(barrier, 1, device_id={"lev": lev + 1}, device_id_type=MESH)

    for r in range(1, n_lon):
        pl.semaphore_signal(barrier, 1, device_id={"lon": lax.rem(lon + r, n_lon)}, device_id_type=MESH)
    pl.semaphore_wait(
        barrier,
        n_lon
        + has_peer.astype(jnp.int32)
        + (lev > 0).astype(jnp.int32)
        + (lev < n_lev - 1).astype(jnp.int32),
    )

    state = (even, odd, even)

    def chip_copy(s, g):
        origin = tracer if s == 0 else state[s]
        return pltpu.make_async_remote_copy(
            origin.at[plane(0), :, rows(g), :],
            chip.at[s, :, rows(g), :],
            chip_send.at[s, g],
            chip_recv.at[s, g],
            device_id={"lat": peer},
            device_id_type=MESH,
        )

    def pair_copy(s):
        origin = tracer if s == 0 else state[s]
        return pltpu.make_async_remote_copy(
            origin.at[plane(planes - 1)],
            pair.at[s],
            pair_send.at[s],
            pair_recv.at[s],
            device_id={"lat": partner},
            device_id_type=MESH,
        )

    def span(part):
        return pl.ds(rest, others) if part else pl.ds(first, 1)

    def k_copy(s, part, side):
        return pltpu.make_async_remote_copy(
            state[s].at[span(part), :, 0 if side else depth - 1, :],
            edge_k.at[s, side, span(part)],
            k_send.at[s, part, side],
            k_recv.at[s, part, side],
            device_id={"lev": lev - 1 if side else lev + 1},
            device_id_type=MESH,
        )

    def i_copy(s, part, side):
        return pltpu.make_async_remote_copy(
            state[s].at[span(part), 0 if side else length - 1],
            edge_i.at[s, side, span(part)],
            i_send.at[s, part, side],
            i_recv.at[s, part, side],
            device_id={"lon": lon - 1 if side else lon + 1},
            device_id_type=MESH,
        )

    def has(index, count, side):
        return index > 0 if side else index < count - 1

    def edges(action, s, part):
        for side in (0, 1):
            there = 1 - side if action == "wait_recv" else side

            @pl.when(has(lev, n_lev, there))
            def _(side=side):
                getattr(k_copy(s, part, side), action)()

            @pl.when(has(lon, n_lon, there))
            def _(side=side):
                getattr(i_copy(s, part, side), action)()

    @pl.when(has_peer)
    def _():
        for g in groups:
            chip_copy(0, g).start()

    pair_copy(0).start()

    def clear(ref, count):
        def one(i, _):
            ref[i] = jnp.zeros(ref.shape[1:], jnp.float32)
            return _

        lax.fori_loop(0, count, one, 0)

    @pl.when(jnp.logical_not(has_peer))
    def _():
        for s in range(STEPS):
            clear(chip.at[s], length)

    for side in (0, 1):

        @pl.when(jnp.logical_not(has(lev, n_lev, 1 - side)))
        def _(side=side):
            for s in range(STEPS):
                clear(edge_k.at[s, side], planes)

        @pl.when(jnp.logical_not(has(lon, n_lon, 1 - side)))
        def _(side=side):
            for s in range(STEPS):
                clear(edge_i.at[s, side], planes)

    def loader(ref, *lead):
        return lambda i, g: ref[(*lead, i, rows(g), slice(None))]

    def advance(s, p, which, near, far, sums=False):
        j = plane(p)
        target = end if s == STEPS - 1 else state[s + 1]

        def store(i, g, value):
            target[j, i, rows(g), :] = value

        return sweep(
            length,
            which,
            total,
            loader(state[s], j),
            near,
            far,
            lambda base: edge_k[s, 0, j, pl.ds(base, ROWS), :],
            lambda base: edge_k[s, 1, j, pl.ds(base, ROWS), :],
            lambda g: edge_i[s, 0, j, rows(g), :],
            lambda g: edge_i[s, 1, j, rows(g), :],
            loader(scaled, j),
            loader(end, j),
            store,
            sums,
        )

    def spread_of(j, which, sums):
        means = [v * (1.0 / length) for v in sums]

        def one(i, so_far):
            out = []
            for n, g in enumerate(which):
                d = end[j, i, rows(g), :] - means[n]
                out.append(so_far[n] + d * d)
            return out

        return means, along(length, one, [jnp.zeros((ROWS, 128), jnp.float32) for _ in which])

    def combined(own, arrived):
        means = [own[0], *(a[0] for a in arrived)]
        mean = functools.reduce(jnp.add, means) * (1.0 / n_lon)
        off = functools.reduce(jnp.add, [(m - mean) * (m - mean) for m in means])
        squares = functools.reduce(jnp.add, [own[1], *(a[1] for a in arrived)])
        variance = (squares + off * float(length)) * (1.0 / (length * n_lon))
        return mean, lax.rsqrt(variance + 0.0001)

    def scale(j, which, pairs):
        def one(i, carry):
            for g, (mean, factor) in zip(which, pairs):
                scaled[j, i, rows(g), :] = (end[j, i, rows(g), :] - mean) * factor
            return carry

        along(length, one, 0)

    def sum_copy(r):
        return pltpu.make_async_remote_copy(
            mine,
            theirs.at[r - 1],
            sum_send.at[r - 1],
            sum_recv.at[r - 1],
            device_id={"lon": lax.rem(lon + r, n_lon)},
            device_id_type=MESH,
        )

    def sum_0_copy(r, g):
        return pltpu.make_async_remote_copy(
            mine_0.at[g],
            theirs_0.at[r - 1, g],
            sum_0_send.at[r - 1, g],
            sum_0_recv.at[r - 1, g],
            device_id={"lon": lax.rem(lon + r, n_lon)},
            device_id_type=MESH,
        )

    for p in (*range(1, planes), 0):
        load(0, p).wait()
    for part in (1, 0):
        edges("start", 0, part)

    for s in range(STEPS):
        closing = s == STEPS - 1
        edges("wait_recv", s, 1)
        if s == 1:
            for part in (1, 0):
                edges("wait_send", 0, part)
        for p in range(1, planes):
            j = plane(p)
            if s == 0:
                load(1, p).wait()
                load(2, p).wait()
            if p == planes - 1:
                pair_copy(s).wait_recv()
                far = loader(pair, s)
            else:
                far = loader(state[s], plane(p + 1))
            sums = advance(s, p, groups, loader(state[s], plane(p - 1)), far, closing)
            if closing:
                means, squares = spread_of(j, groups, sums)
                for g in groups:
                    mine[0, p - 1, rows(g), :] = means[g]
                    mine[1, p - 1, rows(g), :] = squares[g]
        if closing:
            for r in range(1, n_lon):
                sum_copy(r).start()
            for r in range(1, n_lon):
                sum_copy(r).wait_recv()
            for p in range(1, planes):
                pairs = []
                for g in groups:
                    own = [mine[n, p - 1, rows(g), :] for n in (0, 1)]
                    rest_of = [[theirs[r, n, p - 1, rows(g), :] for n in (0, 1)] for r in range(n_lon - 1)]
                    pairs.append(combined(own, rest_of))
                scale(plane(p), groups, pairs)
        else:
            edges("start", s + 1, 1)
            pair_copy(s + 1).start()
        edges("wait_recv", s, 0)
        if s == 0:
            load(1, 0).wait()
            load(2, 0).wait()
        for g in groups:

            @pl.when(has_peer)
            def _(g=g):
                chip_copy(s, g).wait_recv()

            sums = advance(s, 0, [g], loader(chip, s), loader(state[s], plane(1)), closing)
            if closing:
                means, squares = spread_of(first, [g], sums)
                mine_0[g, 0] = means[0]
                mine_0[g, 1] = squares[0]
                for r in range(1, n_lon):
                    sum_0_copy(r, g).start()
                for r in range(1, n_lon):
                    sum_0_copy(r, g).wait_recv()
                arrived = [[theirs_0[r, g, n] for n in (0, 1)] for r in range(n_lon - 1)]
                scale(first, [g], [combined([means[0], squares[0]], arrived)])
            else:

                @pl.when(has_peer)
                def _(g=g):
                    chip_copy(s + 1, g).start()

        if not closing:
            edges("start", s + 1, 0)

    for s in range(STEPS):
        pair_copy(s).wait_send()

        @pl.when(has_peer)
        def _(s=s):
            for g in groups:
                chip_copy(s, g).wait_send()

        if s > 0:
            for part in (1, 0):
                edges("wait_send", s, part)
    for r in range(1, n_lon):
        sum_copy(r).wait_send()
        for g in groups:
            sum_0_copy(r, g).wait_send()


def hand_out(a, b, a_out, b_out, sem):
    copies = []
    for j in range(a.shape[0]):
        copies.append(pltpu.make_async_copy(a.at[j], a_out.at[j], sem.at[0, j]))
        copies.append(pltpu.make_async_copy(b.at[j], b_out.at[j], sem.at[1, j]))
    for c in copies:
        c.start()
    for c in copies:
        c.wait()


def shards(sizes, tracer, conductance, source):
    planes, length, depth, members = tracer.shape
    f32 = jnp.float32
    total = depth // ROWS
    lines = sizes[1] - 1
    dma = pltpu.SemaphoreType.DMA
    end, scaled = pl.pallas_call(
        functools.partial(march, sizes),
        out_shape=[pltpu.VMEM(tracer.shape, f32)] * 2,
        in_specs=[pl.BlockSpec(memory_space=pltpu.HBM)] * 3,
        out_specs=[pl.BlockSpec(memory_space=pltpu.VMEM)] * 2,
        scratch_shapes=[
            pltpu.VMEM(tracer.shape, f32),
            pltpu.VMEM(tracer.shape, f32),
            pltpu.VMEM((STEPS, length, depth, members), f32),
            pltpu.VMEM((STEPS, length, depth, members), f32),
            pltpu.VMEM((STEPS, 2, planes, length, members), f32),
            pltpu.VMEM((STEPS, 2, planes, depth, members), f32),
            pltpu.VMEM((2, planes - 1, depth, members), f32),
            pltpu.VMEM((lines, 2, planes - 1, depth, members), f32),
            pltpu.VMEM((total, 2, ROWS, members), f32),
            pltpu.VMEM((lines, total, 2, ROWS, members), f32),
            dma((3, planes)),
            dma((STEPS, total)),
            dma((STEPS, total)),
            dma((STEPS,)),
            dma((STEPS,)),
            dma((STEPS, 2, 2)),
            dma((STEPS, 2, 2)),
            dma((STEPS, 2, 2)),
            dma((STEPS, 2, 2)),
            dma((lines,)),
            dma((lines,)),
            dma((lines, total)),
            dma((lines, total)),
        ],
        compiler_params=pltpu.CompilerParams(
            collective_id=0, has_side_effects=True, vmem_limit_bytes=36 << 20
        ),
        name="march",
    )(tracer, conductance, source)
    scaled, end = pl.pallas_call(
        hand_out,
        out_shape=[jax.ShapeDtypeStruct(tracer.shape, f32)] * 2,
        in_specs=[pl.BlockSpec(memory_space=pltpu.VMEM)] * 2,
        out_specs=[pl.BlockSpec(memory_space=pltpu.HBM)] * 2,
        scratch_shapes=[dma((2, planes))],
        compiler_params=pltpu.CompilerParams(vmem_limit_bytes=1 << 20),
        name="hand_out",
    )(scaled, end)
    return scaled, end


def solution(mesh):
    sizes = tuple(mesh.shape[a] for a in ("lat", "lon", "lev"))
    placed = P("lat", "lon", "lev", None)
    return jax.shard_map(
        functools.partial(shards, sizes),
        mesh=mesh,
        in_specs=(placed,) * 3,
        out_specs=(placed, placed),
        check_vma=False,
    )
```

profile of v0, /device:TPU:1, one launch (start us, length us, event | category | flops | bytes accessed | tf_op | source)
XLA Modules:
  0.0 86.0 jit_solution(776263660047858170)
XLA Ops:
  0.6 79.4 %march.1 = (f32[4,128,32,128]{3,2,1,0:T(8,128)S(1)}, f32[4,128,32,128]{3,2,1,0:T(8,128)S(1)}) custom-call(f32[4,128,32,128]{3,2,1,0:T(8,128)} %tracer.1, f32[4,128,32,128]{3,2,1,0:T(8,128)} %conductance.1, f32[4,128,32,128]{3,2,1,0:T(8,128)} %source.1), custom_call_target="tpu_custom_call" | custom-call | tf_op jit(solution)/shard_map/march/pallas_call | solution.py:428
  80.1 5.9 %hand_out.1 = (f32[4,128,32,128]{3,2,1,0:T(8,128)}, f32[4,128,32,128]{3,2,1,0:T(8,128)}) custom-call(f32[4,128,32,128]{3,2,1,0:T(8,128)S(1)} %get-tuple-element.4.a, f32[4,128,32,128]{3,2,1,0:T(8,128)S(1)} %get-tuple-element.5.b), custom_call_target="tpu_custom_call" | custom-call | tf_op jit(solution)/shard_map/hand_out/pallas_call | solution.py:463
where the time goes:
time: 87.4 us; the launch traced here: 86 us
  Pallas kernels  85.4 us (98%)
    pallas_call x1, Pallas kernels, shards(): pl.pallas_call(functools.partial(march, sizes), out_shape=[pltpu.VMEM(tra...  79.4 us
    pallas_call x1, Pallas kernels, shards(): pl.pallas_call(hand_out, out_shape=[jax.ShapeDtypeStruct(tracer.shape, f3...  5.92 us

commit v1 on v0

--- a/solution.py
+++ b/solution.py
@@ -12,13 +12,13 @@
 MESH = pl.DeviceIdType.MESH
 
 
-def sweep(length, groups, total, centre, near, far, low, high, before, after, held, added, store, sums):
+def sweep(start, length, groups, total, centre, near, far, low, high, before, after, held, added, store, sums):
     row = lax.broadcasted_iota(jnp.int32, (ROWS, 128), 0)
     first, last = row == 0, row == ROWS - 1
 
     def block(t, carry, closing):
         previous, current, so_far = carry
-        base = t * ROWS if closing else pl.multiple_of(t * ROWS, ROWS)
+        base = start + t * ROWS if closing else pl.multiple_of(start + t * ROWS, ROWS)
         lows = low(base) if 0 in groups else None
         highs = high(base) if total - 1 in groups else None
         for q in range(ROWS):
@@ -46,13 +46,12 @@
                 value = current[n] + held(i, g) * spread + added(i, g)
                 store(i, g, value)
                 done.append(value)
-            if sums:
+            if sums is not None:
                 so_far = [a + b for a, b in zip(so_far, done)]
             previous, current = current, following
         return previous, current, so_far
 
-    zeros = [jnp.zeros((ROWS, 128), jnp.float32) for _ in groups] if sums else []
-    carry = ([before(g) for g in groups], [centre(0, g) for g in groups], zeros)
+    carry = ([before(g) for g in groups], [centre(start, g) for g in groups], sums or [])
     blocks = length // ROWS
     carry = lax.fori_loop(0, blocks - 1, lambda t, c: block(t, c, False), carry)
     return block(blocks - 1, carry, True)[2]
@@ -122,52 +121,48 @@
         a, b = ((tracer, even), (conductance, scaled), (source, end))[n]
         return pltpu.make_async_copy(a.at[plane(p)], b.at[plane(p)], load_sem.at[n, p])
 
-    for n in range(3):
-        for p in (*range(1, planes), 0):
-            load(n, p).start()
+    load(0, 0).start()
 
     barrier = pltpu.get_barrier_semaphore()
-    pl.semaphore_signal(barrier, 1, device_id={"lat": partner}, device_id_type=MESH)
+    signal = functools.partial(pl.semaphore_signal, barrier, 1, device_id_type=MESH)
+    signal(device_id={"lat": partner})
+    for r in range(1, n_lon):
+        signal(device_id={"lon": lax.rem(lon + r, n_lon)})
 
     @pl.when(has_peer)
     def _():
-        pl.semaphore_signal(barrier, 1, device_id={"lat": peer}, device_id_type=MESH)
+        signal(device_id={"lat": peer})
 
     @pl.when(lev > 0)
     def _():
-        pl.semaphore_signal(barrier, 1, device_id={"lev": lev - 1}, device_id_type=MESH)
+        signal(device_id={"lev": lev - 1})
 
     @pl.when(lev < n_lev - 1)
     def _():
-        pl.semaphore_signal(barrier, 1, device_id={"lev": lev + 1}, device_id_type=MESH)
-
-    for r in range(1, n_lon):
-        pl.semaphore_signal(barrier, 1, device_id={"lon": lax.rem(lon + r, n_lon)}, device_id_type=MESH)
-    pl.semaphore_wait(
-        barrier,
-        n_lon
-        + has_peer.astype(jnp.int32)
-        + (lev > 0).astype(jnp.int32)
-        + (lev < n_lev - 1).astype(jnp.int32),
-    )
+        signal(device_id={"lev": lev + 1})
+
+    pl.semaphore_wait(barrier, n_lon + sum(c.astype(jnp.int32) for c in (has_peer, lev > 0, lev < n_lev - 1)))
 
     state = (even, odd, even)
 
-    def chip_copy(s, g):
-        origin = tracer if s == 0 else state[s]
+    def pieces(s, g):
+        cuts = 4 if s == STEPS - 1 and g == total - 1 else 1
+        return [(g + c, c * (length // cuts), length // cuts) for c in range(cuts)]
+
+    def chip_copy(s, g, piece):
+        number, start, count = piece
         return pltpu.make_async_remote_copy(
-            origin.at[plane(0), :, rows(g), :],
-            chip.at[s, :, rows(g), :],
-            chip_send.at[s, g],
-            chip_recv.at[s, g],
+            state[s].at[first, pl.ds(start, count), rows(g), :],
+            chip.at[s, pl.ds(start, count), rows(g), :],
+            chip_send.at[s, number],
+            chip_recv.at[s, number],
             device_id={"lat": peer},
             device_id_type=MESH,
         )
 
     def pair_copy(s):
-        origin = tracer if s == 0 else state[s]
         return pltpu.make_async_remote_copy(
-            origin.at[plane(planes - 1)],
+            (tracer if s == 0 else state[s]).at[plane(planes - 1)],
             pair.at[s],
             pair_send.at[s],
             pair_recv.at[s],
@@ -213,12 +208,20 @@
             def _(side=side):
                 getattr(i_copy(s, part, side), action)()
 
-    @pl.when(has_peer)
-    def _():
-        for g in groups:
-            chip_copy(0, g).start()
-
+    def chip_all(action, s, which):
+        @pl.when(has_peer)
+        def _():
+            for g in which:
+                for piece in pieces(s, g):
+                    getattr(chip_copy(s, g, piece), action)()
+
+    load(0, 0).wait()
+    chip_all("start", 0, groups)
     pair_copy(0).start()
+    for n in range(3):
+        for p in (*range(1, planes), 0):
+            if n or p:
+                load(n, p).start()
 
     def clear(ref, count):
         def one(i, _):
@@ -247,41 +250,49 @@
     def loader(ref, *lead):
         return lambda i, g: ref[(*lead, i, rows(g), slice(None))]
 
-    def advance(s, p, which, near, far, sums=False):
+    def advance(s, p, which, near, far, sums=None, start=0, count=length):
         j = plane(p)
+        centre = loader(state[s], j)
         target = end if s == STEPS - 1 else state[s + 1]
 
         def store(i, g, value):
             target[j, i, rows(g), :] = value
 
         return sweep(
-            length,
+            start,
+            count,
             which,
             total,
-            loader(state[s], j),
+            centre,
             near,
             far,
             lambda base: edge_k[s, 0, j, pl.ds(base, ROWS), :],
             lambda base: edge_k[s, 1, j, pl.ds(base, ROWS), :],
-            lambda g: edge_i[s, 0, j, rows(g), :],
-            lambda g: edge_i[s, 1, j, rows(g), :],
+            lambda g: centre(start - 1, g) if start else edge_i[s, 0, j, rows(g), :],
+            lambda g: centre(start + count, g) if start + count < length else edge_i[s, 1, j, rows(g), :],
             loader(scaled, j),
             loader(end, j),
             store,
             sums,
         )
 
-    def spread_of(j, which, sums):
-        means = [v * (1.0 / length) for v in sums]
+    def spread_of(j, which, sums, start, count):
+        means = [v * (1.0 / count) for v in sums]
 
         def one(i, so_far):
             out = []
             for n, g in enumerate(which):
-                d = end[j, i, rows(g), :] - means[n]
+                d = end[j, start + i, rows(g), :] - means[n]
                 out.append(so_far[n] + d * d)
             return out
 
-        return means, along(length, one, [jnp.zeros((ROWS, 128), jnp.float32) for _ in which])
+        return means, along(count, one, nothing(which))
+
+    def merged(one, other, start, count):
+        (mean, squares), (mean_2, squares_2) = one, other
+        off = mean_2 - mean
+        share = count / (start + count)
+        return mean + off * share, squares + squares_2 + off * off * (start * share)
 
     def combined(own, arrived):
         means = [own[0], *(a[0] for a in arrived)]
@@ -319,15 +330,36 @@
             device_id_type=MESH,
         )
 
-    for p in (*range(1, planes), 0):
+    def nothing(which):
+        return [jnp.zeros((ROWS, 128), jnp.float32) for _ in which]
+
+    for p in range(1, planes):
         load(0, p).wait()
     for part in (1, 0):
         edges("start", 0, part)
+
+    def scale_rest():
+        for r in range(1, n_lon):
+            sum_copy(r).wait_recv()
+        for p in range(1, planes):
+            pairs = []
+            for g in groups:
+                own = [mine[n, p - 1, rows(g), :] for n in (0, 1)]
+                arrived = [[theirs[r, n, p - 1, rows(g), :] for n in (0, 1)] for r in range(n_lon - 1)]
+                pairs.append(combined(own, arrived))
+            scale(plane(p), groups, pairs)
+
+    def scale_0(g):
+        for r in range(1, n_lon):
+            sum_0_copy(r, g).wait_recv()
+        arrived = [[theirs_0[r, g, n] for n in (0, 1)] for r in range(n_lon - 1)]
+        scale(first, [g], [combined([mine_0[g, n] for n in (0, 1)], arrived)])
 
     for s in range(STEPS):
         closing = s == STEPS - 1
         edges("wait_recv", s, 1)
         if s == 1:
+            pair_copy(0).wait_send()
             for part in (1, 0):
                 edges("wait_send", 0, part)
         for p in range(1, planes):
@@ -340,24 +372,15 @@
                 far = loader(pair, s)
             else:
                 far = loader(state[s], plane(p + 1))
-            sums = advance(s, p, groups, loader(state[s], plane(p - 1)), far, closing)
+            sums = advance(s, p, groups, loader(state[s], plane(p - 1)), far, nothing(groups) if closing else None)
             if closing:
-                means, squares = spread_of(j, groups, sums)
+                means, squares = spread_of(j, groups, sums, 0, length)
                 for g in groups:
                     mine[0, p - 1, rows(g), :] = means[g]
                     mine[1, p - 1, rows(g), :] = squares[g]
         if closing:
             for r in range(1, n_lon):
                 sum_copy(r).start()
-            for r in range(1, n_lon):
-                sum_copy(r).wait_recv()
-            for p in range(1, planes):
-                pairs = []
-                for g in groups:
-                    own = [mine[n, p - 1, rows(g), :] for n in (0, 1)]
-                    rest_of = [[theirs[r, n, p - 1, rows(g), :] for n in (0, 1)] for r in range(n_lon - 1)]
-                    pairs.append(combined(own, rest_of))
-                scale(plane(p), groups, pairs)
         else:
             edges("start", s + 1, 1)
             pair_copy(s + 1).start()
@@ -366,42 +389,43 @@
             load(1, 0).wait()
             load(2, 0).wait()
         for g in groups:
-
-            @pl.when(has_peer)
-            def _(g=g):
-                chip_copy(s, g).wait_recv()
-
-            sums = advance(s, 0, [g], loader(chip, s), loader(state[s], plane(1)), closing)
+            if s == 1:
+                chip_all("wait_send", 0, [g])
+            for piece in pieces(s, g):
+                _, start, count = piece
+
+                @pl.when(has_peer)
+                def _(g=g, piece=piece):
+                    chip_copy(s, g, piece).wait_recv()
+
+                near, far = loader(chip, s), loader(state[s], plane(1))
+                sums = advance(s, 0, [g], near, far, nothing([g]) if closing else None, start, count)
+                if closing:
+                    (mean,), (squares,) = spread_of(first, [g], sums, start, count)
+                    line = merged(line, (mean, squares), start, count) if start else (mean, squares)
+                if closing and g == total - 1 and start == 0:
+                    scale_0(g - 1)
             if closing:
-                means, squares = spread_of(first, [g], sums)
-                mine_0[g, 0] = means[0]
-                mine_0[g, 1] = squares[0]
+                for n in (0, 1):
+                    mine_0[g, n] = line[n]
                 for r in range(1, n_lon):
                     sum_0_copy(r, g).start()
-                for r in range(1, n_lon):
-                    sum_0_copy(r, g).wait_recv()
-                arrived = [[theirs_0[r, g, n] for n in (0, 1)] for r in range(n_lon - 1)]
-                scale(first, [g], [combined([means[0], squares[0]], arrived)])
+                if g == 0:
+                    scale_rest()
+                elif g < total - 1:
+                    scale_0(g - 1)
+                else:
+                    scale_0(g)
             else:
-
-                @pl.when(has_peer)
-                def _(g=g):
-                    chip_copy(s + 1, g).start()
-
+                chip_all("start", s + 1, [g])
         if not closing:
             edges("start", s + 1, 0)
 
-    for s in range(STEPS):
+    for s in range(1, STEPS):
         pair_copy(s).wait_send()
-
-        @pl.when(has_peer)
-        def _(s=s):
-            for g in groups:
-                chip_copy(s, g).wait_send()
-
-        if s > 0:
-            for part in (1, 0):
-                edges("wait_send", s, part)
+        chip_all("wait_send", s, groups)
+        for part in (1, 0):
+            edges("wait_send", s, part)
     for r in range(1, n_lon):
         sum_copy(r).wait_send()
         for g in groups:
@@ -442,8 +466,8 @@
             pltpu.VMEM((total, 2, ROWS, members), f32),
             pltpu.VMEM((lines, total, 2, ROWS, members), f32),
             dma((3, planes)),
-            dma((STEPS, total)),
-            dma((STEPS, total)),
+            dma((STEPS, total + 3)),
+            dma((STEPS, total + 3)),
             dma((STEPS,)),
             dma((STEPS,)),
             dma((STEPS, 2, 2)),

time: 87.4 us -> 85.6 us (0.979); the launches traced: 86 us -> 85.5 us
  no operation moved by 1% of the time
where the time goes in v1:
time: 85.6 us; the launch traced here: 85.5 us
  Pallas kernels  84.8 us (99%)
    pallas_call x1, Pallas kernels, shards(): pl.pallas_call(functools.partial(march, sizes), out_shape=[pltpu.VMEM(tra...  78.9 us
    pallas_call x1, Pallas kernels, shards(): pl.pallas_call(hand_out, out_shape=[jax.ShapeDtypeStruct(tracer.shape, f3...  5.92 us

profile of v1, /device:TPU:1, one launch (start us, length us, event | category | flops | bytes accessed | tf_op | source)
XLA Modules:
  0.0 85.5 jit_solution(12825731278250628405)
XLA Ops:
  0.6 78.9 %march.1 = (f32[4,128,32,128]{3,2,1,0:T(8,128)S(1)}, f32[4,128,32,128]{3,2,1,0:T(8,128)S(1)}) custom-call(f32[4,128,32,128]{3,2,1,0:T(8,128)} %tracer.1, f32[4,128,32,128]{3,2,1,0:T(8,128)} %conductance.1, f32[4,128,32,128]{3,2,1,0:T(8,128)} %source.1), custom_call_target="tpu_custom_call" | custom-call | tf_op jit(solution)/shard_map/march/pallas_call | solution.py:452
  79.5 5.9 %hand_out.1 = (f32[4,128,32,128]{3,2,1,0:T(8,128)}, f32[4,128,32,128]{3,2,1,0:T(8,128)}) custom-call(f32[4,128,32,128]{3,2,1,0:T(8,128)S(1)} %get-tuple-element.4.a, f32[4,128,32,128]{3,2,1,0:T(8,128)S(1)} %get-tuple-element.5.b), custom_call_target="tpu_custom_call" | custom-call | tf_op jit(solution)/shard_map/hand_out/pallas_call | solution.py:487

commit v2 on v1

--- a/solution.py
+++ b/solution.py
@@ -83,7 +83,11 @@
     theirs,
     mine_0,
     theirs_0,
+    gather,
+    across,
+    go,
     load_sem,
+    first_sem,
     chip_send,
     chip_recv,
     pair_send,
@@ -121,27 +125,41 @@
         a, b = ((tracer, even), (conductance, scaled), (source, end))[n]
         return pltpu.make_async_copy(a.at[plane(p)], b.at[plane(p)], load_sem.at[n, p])
 
-    load(0, 0).start()
+    def load_first(g):
+        return pltpu.make_async_copy(
+            tracer.at[first, :, rows(g), :], even.at[first, :, rows(g), :], first_sem.at[g]
+        )
+
+    for g in groups:
+        load_first(g).start()
 
     barrier = pltpu.get_barrier_semaphore()
-    signal = functools.partial(pl.semaphore_signal, barrier, 1, device_id_type=MESH)
-    signal(device_id={"lat": partner})
-    for r in range(1, n_lon):
-        signal(device_id={"lon": lax.rem(lon + r, n_lon)})
+    signal = functools.partial(pl.semaphore_signal, inc=1, device_id_type=MESH)
+
+    def greet(semaphore):
+        for r in range(1, n_lon):
+            signal(semaphore, device_id={"lon": lax.rem(lon + r, n_lon)})
+
+        @pl.when(lev > 0)
+        def _():
+            signal(semaphore, device_id={"lev": lev - 1})
+
+        @pl.when(lev < n_lev - 1)
+        def _():
+            signal(semaphore, device_id={"lev": lev + 1})
+
+    beside = n_lon - 1 + (lev > 0).astype(jnp.int32) + (lev < n_lev - 1).astype(jnp.int32)
+    signal(barrier, device_id={"lat": partner})
 
     @pl.when(has_peer)
     def _():
-        signal(device_id={"lat": peer})
-
-    @pl.when(lev > 0)
-    def _():
-        signal(device_id={"lev": lev - 1})
-
-    @pl.when(lev < n_lev - 1)
-    def _():
-        signal(device_id={"lev": lev + 1})
-
-    pl.semaphore_wait(barrier, n_lon + sum(c.astype(jnp.int32) for c in (has_peer, lev > 0, lev < n_lev - 1)))
+        signal(barrier, device_id={"lat": peer})
+
+    @pl.when(jnp.logical_not(has_peer))
+    def _():
+        greet(barrier)
+
+    pl.semaphore_wait(barrier, jnp.where(has_peer, 2, 1 + beside))
 
     state = (even, odd, even)
 
@@ -215,8 +233,9 @@
                 for piece in pieces(s, g):
                     getattr(chip_copy(s, g, piece), action)()
 
-    load(0, 0).wait()
-    chip_all("start", 0, groups)
+    for g in groups:
+        load_first(g).wait()
+        chip_all("start", 0, [g])
     pair_copy(0).start()
     for n in range(3):
         for p in (*range(1, planes), 0):
@@ -246,6 +265,30 @@
         def _(side=side):
             for s in range(STEPS):
                 clear(edge_i.at[s, side], planes)
+
+    half = n_lat // 2
+    low_half = lat < half
+    depth_in = jnp.where(low_half, lat, n_lat - 1 - lat)
+    inward = jnp.where(low_half, lat + 1, lat - 1)
+    outward = jnp.where(low_half, lat - 1, lat + 1)
+
+    @pl.when(depth_in < half - 1)
+    def _():
+        pl.semaphore_wait(gather, 1)
+
+    @pl.when(depth_in > 0)
+    def _():
+        signal(gather, device_id={"lat": outward})
+        pl.semaphore_wait(go, 1)
+
+    @pl.when(depth_in == 0)
+    def _():
+        greet(across)
+        pl.semaphore_wait(across, beside)
+
+    @pl.when(depth_in < half - 1)
+    def _():
+        signal(go, device_id={"lat": inward})
 
     def loader(ref, *lead):
         return lambda i, g: ref[(*lead, i, rows(g), slice(None))]
@@ -408,7 +451,7 @@
             if closing:
                 for n in (0, 1):
                     mine_0[g, n] = line[n]
-                for r in range(1, n_lon):
+                for r in (*range(2, n_lon), 1):
                     sum_0_copy(r, g).start()
                 if g == 0:
                     scale_rest()
@@ -465,7 +508,11 @@
             pltpu.VMEM((lines, 2, planes - 1, depth, members), f32),
             pltpu.VMEM((total, 2, ROWS, members), f32),
             pltpu.VMEM((lines, total, 2, ROWS, members), f32),
+            pltpu.SemaphoreType.REGULAR,
+            pltpu.SemaphoreType.REGULAR,
+            pltpu.SemaphoreType.REGULAR,
             dma((3, planes)),
+            dma((total,)),
             dma((STEPS, total + 3)),
             dma((STEPS, total + 3)),
             dma((STEPS,)),

time: 85.6 us -> 84.6 us (0.988)
  Pallas kernels: 84.8 us -> 83.9 us
    pallas_call x1, Pallas kernels: 78.9 us -> 77.9 us  [shards(): pl.pallas_call(functools.partial(march, sizes), out_shape=[pltpu.VMEM(tra...]
where the time goes in v2:
time: 84.6 us; the launch traced here: 84.5 us
  Pallas kernels  83.9 us (99%)
    pallas_call x1, Pallas kernels, shards(): pl.pallas_call(functools.partial(march, sizes), out_shape=[pltpu.VMEM(tra...  77.9 us
    pallas_call x1, Pallas kernels, shards(): pl.pallas_call(hand_out, out_shape=[jax.ShapeDtypeStruct(tracer.shape, f3...  5.92 us

profile of v2, /device:TPU:1, one launch (start us, length us, event | category | flops | bytes accessed | tf_op | source)
XLA Modules:
  0.0 84.5 jit_solution(14543482951097977309)
XLA Ops:
  0.6 77.9 %march.1 = (f32[4,128,32,128]{3,2,1,0:T(8,128)S(1)}, f32[4,128,32,128]{3,2,1,0:T(8,128)S(1)}) custom-call(f32[4,128,32,128]{3,2,1,0:T(8,128)} %tracer.1, f32[4,128,32,128]{3,2,1,0:T(8,128)} %conductance.1, f32[4,128,32,128]{3,2,1,0:T(8,128)} %source.1), custom_call_target="tpu_custom_call" | custom-call | tf_op jit(solution)/shard_map/march/pallas_call | solution.py:495
  78.6 5.9 %hand_out.1 = (f32[4,128,32,128]{3,2,1,0:T(8,128)}, f32[4,128,32,128]{3,2,1,0:T(8,128)}) custom-call(f32[4,128,32,128]{3,2,1,0:T(8,128)S(1)} %get-tuple-element.4.a, f32[4,128,32,128]{3,2,1,0:T(8,128)S(1)} %get-tuple-element.5.b), custom_call_target="tpu_custom_call" | custom-call | tf_op jit(solution)/shard_map/hand_out/pallas_call | solution.py:534

commit v3 on v2

--- a/solution.py
+++ b/solution.py
@@ -73,6 +73,7 @@
     source,
     end,
     scaled,
+    closing_line,
     even,
     odd,
     chip,
@@ -87,7 +88,6 @@
     across,
     go,
     load_sem,
-    first_sem,
     chip_send,
     chip_recv,
     pair_send,
@@ -125,13 +125,6 @@
         a, b = ((tracer, even), (conductance, scaled), (source, end))[n]
         return pltpu.make_async_copy(a.at[plane(p)], b.at[plane(p)], load_sem.at[n, p])
 
-    def load_first(g):
-        return pltpu.make_async_copy(
-            tracer.at[first, :, rows(g), :], even.at[first, :, rows(g), :], first_sem.at[g]
-        )
-
-    for g in groups:
-        load_first(g).start()
 
     barrier = pltpu.get_barrier_semaphore()
     signal = functools.partial(pl.semaphore_signal, inc=1, device_id_type=MESH)
@@ -149,11 +142,12 @@
             signal(semaphore, device_id={"lev": lev + 1})
 
     beside = n_lon - 1 + (lev > 0).astype(jnp.int32) + (lev < n_lev - 1).astype(jnp.int32)
+
+    @pl.when(has_peer)
+    def _():
+        signal(barrier, device_id={"lat": peer})
+
     signal(barrier, device_id={"lat": partner})
-
-    @pl.when(has_peer)
-    def _():
-        signal(barrier, device_id={"lat": peer})
 
     @pl.when(jnp.logical_not(has_peer))
     def _():
@@ -170,7 +164,7 @@
     def chip_copy(s, g, piece):
         number, start, count = piece
         return pltpu.make_async_remote_copy(
-            state[s].at[first, pl.ds(start, count), rows(g), :],
+            (tracer if s == 0 else state[s]).at[first, pl.ds(start, count), rows(g), :],
             chip.at[s, pl.ds(start, count), rows(g), :],
             chip_send.at[s, number],
             chip_recv.at[s, number],
@@ -233,14 +227,11 @@
                 for piece in pieces(s, g):
                     getattr(chip_copy(s, g, piece), action)()
 
-    for g in groups:
-        load_first(g).wait()
-        chip_all("start", 0, [g])
+    chip_all("start", 0, groups)
     pair_copy(0).start()
     for n in range(3):
         for p in (*range(1, planes), 0):
-            if n or p:
-                load(n, p).start()
+            load(n, p).start()
 
     def clear(ref, count):
         def one(i, _):
@@ -376,7 +367,7 @@
     def nothing(which):
         return [jnp.zeros((ROWS, 128), jnp.float32) for _ in which]
 
-    for p in range(1, planes):
+    for p in range(planes):
         load(0, p).wait()
     for part in (1, 0):
         edges("start", 0, part)
@@ -392,11 +383,14 @@
                 pairs.append(combined(own, arrived))
             scale(plane(p), groups, pairs)
 
-    def scale_0(g):
+    def line_0(g):
         for r in range(1, n_lon):
             sum_0_copy(r, g).wait_recv()
         arrived = [[theirs_0[r, g, n] for n in (0, 1)] for r in range(n_lon - 1)]
-        scale(first, [g], [combined([mine_0[g, n] for n in (0, 1)], arrived)])
+        return combined([mine_0[g, n] for n in (0, 1)], arrived)
+
+    def scale_0(g):
+        scale(first, [g], [line_0(g)])
 
     for s in range(STEPS):
         closing = s == STEPS - 1
@@ -432,8 +426,6 @@
             load(1, 0).wait()
             load(2, 0).wait()
         for g in groups:
-            if s == 1:
-                chip_all("wait_send", 0, [g])
             for piece in pieces(s, g):
                 _, start, count = piece
 
@@ -458,15 +450,17 @@
                 elif g < total - 1:
                     scale_0(g - 1)
                 else:
-                    scale_0(g)
+                    for n, v in enumerate(line_0(g)):
+                        closing_line[n] = v
             else:
                 chip_all("start", s + 1, [g])
         if not closing:
             edges("start", s + 1, 0)
 
+    for s in range(STEPS):
+        chip_all("wait_send", s, groups)
     for s in range(1, STEPS):
         pair_copy(s).wait_send()
-        chip_all("wait_send", s, groups)
         for part in (1, 0):
             edges("wait_send", s, part)
     for r in range(1, n_lon):
@@ -475,13 +469,27 @@
             sum_0_copy(r, g).wait_send()
 
 
-def hand_out(a, b, a_out, b_out, sem):
-    copies = []
-    for j in range(a.shape[0]):
-        copies.append(pltpu.make_async_copy(a.at[j], a_out.at[j], sem.at[0, j]))
-        copies.append(pltpu.make_async_copy(b.at[j], b_out.at[j], sem.at[1, j]))
+def hand_out(scaled, end, line, scaled_out, end_out, last, sem):
+    planes, length, depth, _ = end.shape
+    core = lax.rem(lax.axis_index("lat"), 2)
+    first, way = core * (planes - 1), 1 - 2 * core
+    rows, held = pl.ds(depth - ROWS, ROWS), pl.ds(0, depth - ROWS)
+    copies = [pltpu.make_async_copy(end.at[j], end_out.at[j], sem.at[0, j]) for j in range(planes)]
+    for p in range(1, planes):
+        j = first + way * p
+        copies.append(pltpu.make_async_copy(scaled.at[j], scaled_out.at[j], sem.at[1, p]))
+    copies.append(pltpu.make_async_copy(scaled.at[first, :, held], scaled_out.at[first, :, held], sem.at[1, 0]))
     for c in copies:
         c.start()
+    mean, factor = line[0], line[1]
+
+    def one(i, carry):
+        last[i] = (end[first, i, rows, :] - mean) * factor
+        return carry
+
+    along(length, one, 0)
+    copies.append(pltpu.make_async_copy(last, scaled_out.at[first, :, rows], sem.at[1, planes]))
+    copies[-1].start()
     for c in copies:
         c.wait()
 
@@ -492,11 +500,11 @@
     total = depth // ROWS
     lines = sizes[1] - 1
     dma = pltpu.SemaphoreType.DMA
-    end, scaled = pl.pallas_call(
+    end, scaled, line = pl.pallas_call(
         functools.partial(march, sizes),
-        out_shape=[pltpu.VMEM(tracer.shape, f32)] * 2,
+        out_shape=[pltpu.VMEM(a, f32) for a in (tracer.shape, tracer.shape, (2, ROWS, members))],
         in_specs=[pl.BlockSpec(memory_space=pltpu.HBM)] * 3,
-        out_specs=[pl.BlockSpec(memory_space=pltpu.VMEM)] * 2,
+        out_specs=[pl.BlockSpec(memory_space=pltpu.VMEM)] * 3,
         scratch_shapes=[
             pltpu.VMEM(tracer.shape, f32),
             pltpu.VMEM(tracer.shape, f32),
@@ -512,7 +520,6 @@
             pltpu.SemaphoreType.REGULAR,
             pltpu.SemaphoreType.REGULAR,
             dma((3, planes)),
-            dma((total,)),
             dma((STEPS, total + 3)),
             dma((STEPS, total + 3)),
             dma((STEPS,)),
@@ -534,12 +541,12 @@
     scaled, end = pl.pallas_call(
         hand_out,
         out_shape=[jax.ShapeDtypeStruct(tracer.shape, f32)] * 2,
-        in_specs=[pl.BlockSpec(memory_space=pltpu.VMEM)] * 2,
+        in_specs=[pl.BlockSpec(memory_space=pltpu.VMEM)] * 3,
         out_specs=[pl.BlockSpec(memory_space=pltpu.HBM)] * 2,
-        scratch_shapes=[dma((2, planes))],
-        compiler_params=pltpu.CompilerParams(vmem_limit_bytes=1 << 20),
+        scratch_shapes=[pltpu.VMEM((length, ROWS, members), f32), dma((2, planes + 1))],
+        compiler_params=pltpu.CompilerParams(vmem_limit_bytes=2 << 20),
         name="hand_out",
-    )(scaled, end)
+    )(scaled, end, line)
     return scaled, end
 
 

time: 84.6 us -> 83.6 us (0.988)
  Pallas kernels: 83.9 us -> 82.8 us
    pallas_call x1, Pallas kernels: 77.9 us -> 77 us  [shards(): pl.pallas_call(functools.partial(march, sizes), out_shape=[pltpu.VMEM(a,...]
where the time goes in v3:
time: 83.6 us; the launch traced here: 83.5 us
  Pallas kernels  82.8 us (99%)
    pallas_call x1, Pallas kernels, shards(): pl.pallas_call(functools.partial(march, sizes), out_shape=[pltpu.VMEM(a,...  77 us
    pallas_call x1, Pallas kernels, shards(): pl.pallas_call(hand_out, out_shape=[jax.ShapeDtypeStruct(tracer.shape, f3...  5.89 us

profile of v3, /device:TPU:1, one launch (start us, length us, event | category | flops | bytes accessed | tf_op | source)
XLA Modules:
  0.0 83.5 jit_solution(1687200522317554811)
XLA Ops:
  0.6 77.0 %march.1 = (f32[4,128,32,128]{3,2,1,0:T(8,128)S(1)}, f32[4,128,32,128]{3,2,1,0:T(8,128)S(1)}, f32[2,8,128]{2,1,0:T(8,128)S(1)}) custom-call(f32[4,128,32,128]{3,2,1,0:T(8,128)} %tracer.1, f32[4,128,32,128]{3,2,1,0:T(8,128)} %conductance.1, f32[4,128,32,128]{3,2,1,0:T(8,128)} %source.1), custom_call_target="tpu_custom_call" | custom-call | tf_op jit(solution)/shard_map/march/pallas_call | solution.py:503
  77.6 5.9 %hand_out.1 = (f32[4,128,32,128]{3,2,1,0:T(8,128)}, f32[4,128,32,128]{3,2,1,0:T(8,128)}) custom-call(f32[4,128,32,128]{3,2,1,0:T(8,128)S(1)} %get-tuple-element.5.scaled, f32[4,128,32,128]{3,2,1,0:T(8,128)S(1)} %get-tuple-element.6.end, f32[2,8,128]{2,1,0:T(8,128)S(1)} %get-tuple-element.7.line), custom_call_target="tpu_custom_call" | custom-call | tf_op jit(solution)/shard_map/hand_out/pallas_call | solution.py:541

commit v4 on v3

--- a/solution.py
+++ b/solution.py
@@ -392,6 +392,18 @@
     def scale_0(g):
         scale(first, [g], [line_0(g)])
 
+    def all_sent():
+        for s in range(STEPS):
+            chip_all("wait_send", s, groups)
+        for s in range(1, STEPS):
+            pair_copy(s).wait_send()
+            for part in (1, 0):
+                edges("wait_send", s, part)
+        for r in range(1, n_lon):
+            sum_copy(r).wait_send()
+            for g in groups:
+                sum_0_copy(r, g).wait_send()
+
     for s in range(STEPS):
         closing = s == STEPS - 1
         edges("wait_recv", s, 1)
@@ -450,23 +462,13 @@
                 elif g < total - 1:
                     scale_0(g - 1)
                 else:
+                    all_sent()
                     for n, v in enumerate(line_0(g)):
                         closing_line[n] = v
             else:
                 chip_all("start", s + 1, [g])
         if not closing:
             edges("start", s + 1, 0)
-
-    for s in range(STEPS):
-        chip_all("wait_send", s, groups)
-    for s in range(1, STEPS):
-        pair_copy(s).wait_send()
-        for part in (1, 0):
-            edges("wait_send", s, part)
-    for r in range(1, n_lon):
-        sum_copy(r).wait_send()
-        for g in groups:
-            sum_0_copy(r, g).wait_send()
 
 
 def hand_out(scaled, end, line, scaled_out, end_out, last, sem):

time: 83.6 us -> 83.5 us (level)
  no operation moved by 1% of the time
where the time goes in v4:
time: 83.5 us; the launch traced here: 83.4 us
  Pallas kernels  82.8 us (99%)
    pallas_call x1, Pallas kernels, shards(): pl.pallas_call(functools.partial(march, sizes), out_shape=[pltpu.VMEM(a,...  76.9 us
    pallas_call x1, Pallas kernels, shards(): pl.pallas_call(hand_out, out_shape=[jax.ShapeDtypeStruct(tracer.shape, f3...  5.89 us

profile of v4, /device:TPU:1, one launch (start us, length us, event | category | flops | bytes accessed | tf_op | source)
XLA Modules:
  0.0 83.4 jit_solution(13843010391904983190)
XLA Ops:
  0.6 76.9 %march.1 = (f32[4,128,32,128]{3,2,1,0:T(8,128)S(1)}, f32[4,128,32,128]{3,2,1,0:T(8,128)S(1)}, f32[2,8,128]{2,1,0:T(8,128)S(1)}) custom-call(f32[4,128,32,128]{3,2,1,0:T(8,128)} %tracer.1, f32[4,128,32,128]{3,2,1,0:T(8,128)} %conductance.1, f32[4,128,32,128]{3,2,1,0:T(8,128)} %source.1), custom_call_target="tpu_custom_call" | custom-call | tf_op jit(solution)/shard_map/march/pallas_call | solution.py:505
  77.5 5.9 %hand_out.1 = (f32[4,128,32,128]{3,2,1,0:T(8,128)}, f32[4,128,32,128]{3,2,1,0:T(8,128)}) custom-call(f32[4,128,32,128]{3,2,1,0:T(8,128)S(1)} %get-tuple-element.5.scaled, f32[4,128,32,128]{3,2,1,0:T(8,128)S(1)} %get-tuple-element.6.end, f32[2,8,128]{2,1,0:T(8,128)S(1)} %get-tuple-element.7.line), custom_call_target="tpu_custom_call" | custom-call | tf_op jit(solution)/shard_map/hand_out/pallas_call | solution.py:543

commit v5 on v4

--- a/solution.py
+++ b/solution.py
@@ -161,11 +161,18 @@
         cuts = 4 if s == STEPS - 1 and g == total - 1 else 1
         return [(g + c, c * (length // cuts), length // cuts) for c in range(cuts)]
 
+    def units(s):
+        size = 1 if s == STEPS - 1 else 2
+        return [groups[n : n + size] for n in range(0, total, size)]
+
+    def block(s, g):
+        return pl.ds(ROWS * g, ROWS * len(units(s)[0]))
+
     def chip_copy(s, g, piece):
         number, start, count = piece
         return pltpu.make_async_remote_copy(
-            (tracer if s == 0 else state[s]).at[first, pl.ds(start, count), rows(g), :],
-            chip.at[s, pl.ds(start, count), rows(g), :],
+            (tracer if s == 0 else state[s]).at[first, pl.ds(start, count), block(s, g), :],
+            chip.at[s, pl.ds(start, count), block(s, g), :],
             chip_send.at[s, number],
             chip_recv.at[s, number],
             device_id={"lat": peer},
@@ -227,7 +234,7 @@
                 for piece in pieces(s, g):
                     getattr(chip_copy(s, g, piece), action)()
 
-    chip_all("start", 0, groups)
+    chip_all("start", 0, [u[0] for u in units(0)])
     pair_copy(0).start()
     for n in range(3):
         for p in (*range(1, planes), 0):
@@ -394,7 +401,7 @@
 
     def all_sent():
         for s in range(STEPS):
-            chip_all("wait_send", s, groups)
+            chip_all("wait_send", s, [u[0] for u in units(s)])
         for s in range(1, STEPS):
             pair_copy(s).wait_send()
             for part in (1, 0):
@@ -437,7 +444,8 @@
         if s == 0:
             load(1, 0).wait()
             load(2, 0).wait()
-        for g in groups:
+        for unit in units(s):
+            g = unit[0]
             for piece in pieces(s, g):
                 _, start, count = piece
 
@@ -446,7 +454,7 @@
                     chip_copy(s, g, piece).wait_recv()
 
                 near, far = loader(chip, s), loader(state[s], plane(1))
-                sums = advance(s, 0, [g], near, far, nothing([g]) if closing else None, start, count)
+                sums = advance(s, 0, unit, near, far, nothing([g]) if closing else None, start, count)
                 if closing:
                     (mean,), (squares,) = spread_of(first, [g], sums, start, count)
                     line = merged(line, (mean, squares), start, count) if start else (mean, squares)
@@ -466,7 +474,7 @@
                     for n, v in enumerate(line_0(g)):
                         closing_line[n] = v
             else:
-                chip_all("start", s + 1, [g])
+                chip_all("start", s + 1, [u[0] for u in units(s + 1) if u[0] in unit])
         if not closing:
             edges("start", s + 1, 0)
 

time: 83.5 us -> 83.5 us (level)
  no operation moved by 1% of the time
where the time goes in v5:
time: 83.5 us; the launch traced here: 83.4 us
  Pallas kernels  82.8 us (99%)
    pallas_call x1, Pallas kernels, shards(): pl.pallas_call(functools.partial(march, sizes), out_shape=[pltpu.VMEM(a,...  76.9 us
    pallas_call x1, Pallas kernels, shards(): pl.pallas_call(hand_out, out_shape=[jax.ShapeDtypeStruct(tracer.shape, f3...  5.89 us

profile of v5, /device:TPU:1, one launch (start us, length us, event | category | flops | bytes accessed | tf_op | source)
XLA Modules:
  0.0 83.4 jit_solution(7055442283867594506)
XLA Ops:
  0.6 76.9 %march.1 = (f32[4,128,32,128]{3,2,1,0:T(8,128)S(1)}, f32[4,128,32,128]{3,2,1,0:T(8,128)S(1)}, f32[2,8,128]{2,1,0:T(8,128)S(1)}) custom-call(f32[4,128,32,128]{3,2,1,0:T(8,128)} %tracer.1, f32[4,128,32,128]{3,2,1,0:T(8,128)} %conductance.1, f32[4,128,32,128]{3,2,1,0:T(8,128)} %source.1), custom_call_target="tpu_custom_call" | custom-call | tf_op jit(solution)/shard_map/march/pallas_call | solution.py:513
  77.5 5.9 %hand_out.1 = (f32[4,128,32,128]{3,2,1,0:T(8,128)}, f32[4,128,32,128]{3,2,1,0:T(8,128)}) custom-call(f32[4,128,32,128]{3,2,1,0:T(8,128)S(1)} %get-tuple-element.5.scaled, f32[4,128,32,128]{3,2,1,0:T(8,128)S(1)} %get-tuple-element.6.end, f32[2,8,128]{2,1,0:T(8,128)S(1)} %get-tuple-element.7.line), custom_call_target="tpu_custom_call" | custom-call | tf_op jit(solution)/shard_map/hand_out/pallas_call | solution.py:551
